TPU v7x, 32 devices: a whole 2x2x4 slice. The times are simulated.
32 devices in a mesh: model: 8 (over z, y), fsdp: 4 (over x, core).
Axes of the slice: x: 2, y: 2, z: 4, core: 2. Of those that a mesh axis runs over, the one named last changes fastest.
Arguments:
- tok_ids: int32 [4, 1024], P('fsdp')
- tok_labels: int32 [4, 1024], P('fsdp')
- emb_table: bfloat16 [151936, 896], P(('model', 'fsdp'))
- w_gate: bfloat16 [896, 4864], P('fsdp')
- w_up: bfloat16 [896, 4864], P('fsdp')
- w_down: bfloat16 [4864, 896], P('fsdp')
- gain_in: float32 [896], replicated
- gain_out: float32 [896], replicated
Outputs:
- output 1: float32 [], replicated
- output 2: float32 [151936, 896], P(('model', 'fsdp'))
- output 3: float32 [896, 4864], P('fsdp')
- output 4: float32 [896, 4864], P('fsdp')
- output 5: float32 [4864, 896], P('fsdp')
All inputs are finite; a program needn't handle non-finite values.
Results may differ from a plain program's by a relative error of at most 0.0111091.
Values are sent between devices in bfloat16 or wider.
A program may use at most 1 GiB of HBM per device.

v0:
```python
import jax
import jax.numpy as jnp
from jax import lax
from jax.sharding import PartitionSpec as P

EPS = 1e-6


def rms_scale(values, gain_vec):
    mean_sq = jnp.mean(values * values, axis=-1, keepdims=True)
    return values * lax.rsqrt(mean_sq + EPS) * gain_vec


def mlp_forward(x_emb, gain_in, w_gate, w_up, w_down):
    normed_in, norm_in_back = jax.vjp(lambda values: rms_scale(values, gain_in), x_emb)
    normed_bf = normed_in.astype(jnp.bfloat16)
    gate_f = jnp.dot(normed_bf, w_gate, preferred_element_type=jnp.float32).astype(jnp.bfloat16).astype(jnp.float32)
    up_f = jnp.dot(normed_bf, w_up, preferred_element_type=jnp.float32).astype(jnp.bfloat16).astype(jnp.float32)
    gate_sig = jax.nn.sigmoid(gate_f)
    silu_gate = gate_f * gate_sig
    act_bf = (silu_gate * up_f).astype(jnp.bfloat16)
    mlp_out = jnp.dot(act_bf, w_down, preferred_element_type=jnp.float32).astype(jnp.bfloat16)
    h_res = x_emb + mlp_out.astype(jnp.float32)
    return h_res, (norm_in_back, normed_bf, gate_f, up_f, gate_sig, silu_gate, act_bf)


def mlp_backward(d_hidden, saved, w_gate, w_up, w_down):
    norm_in_back, normed_bf, gate_f, up_f, gate_sig, silu_gate, act_bf = saved
    d_mlp = d_hidden.astype(jnp.bfloat16)
    d_act = jnp.einsum("td,fd->tf", d_mlp, w_down, preferred_element_type=jnp.float32)
    grad_down = jnp.einsum("tf,td->fd", act_bf, d_mlp, preferred_element_type=jnp.float32)
    d_gate = (d_act * up_f * (gate_sig * (1.0 + gate_f * (1.0 - gate_sig)))).astype(jnp.bfloat16)
    d_up = (d_act * silu_gate).astype(jnp.bfloat16)
    grad_gate = jnp.einsum("td,tf->df", normed_bf, d_gate, preferred_element_type=jnp.float32)
    grad_up = jnp.einsum("td,tf->df", normed_bf, d_up, preferred_element_type=jnp.float32)
    d_normed = jnp.einsum("tf,df->td", d_gate, w_gate, preferred_element_type=jnp.float32) + jnp.einsum("tf,df->td", d_up, w_up, preferred_element_type=jnp.float32)
    d_x = d_hidden + norm_in_back(d_normed)[0]
    return d_x, grad_gate, grad_up, grad_down


def solution(mesh):
    fsdp_size = mesh.shape["fsdp"]
    tok_spec = P("fsdp", None)
    row_spec = P(("model", "fsdp"), None)
    weight_spec = P("fsdp", None)

    def device_step(tok_ids, tok_labels, table_shard, gate_shard, up_shard, down_shard, gain_in, gain_out):
        local_count = tok_ids.shape[0] * tok_ids.shape[1]
        num_tokens = local_count * fsdp_size
        table_part = lax.all_gather(table_shard, "fsdp", axis=0, tiled=True)
        w_gate = lax.all_gather(gate_shard, "fsdp", axis=0, tiled=True)
        w_up = lax.all_gather(up_shard, "fsdp", axis=0, tiled=True)
        w_down = lax.all_gather(down_shard, "fsdp", axis=0, tiled=True)
        vocab_part = table_part.shape[0]
        vocab_start = lax.axis_index("model") * vocab_part
        local_ids = tok_ids.reshape(local_count) - vocab_start
        id_inside = (local_ids >= 0) & (local_ids < vocab_part)
        safe_ids = jnp.where(id_inside, local_ids, 0)
        emb_rows = jnp.where(id_inside[:, None], jnp.take(table_part, safe_ids, axis=0), 0)
        x_emb = lax.psum(emb_rows, "model").astype(jnp.float32)
        h_res, saved = mlp_forward(x_emb, gain_in, w_gate, w_up, w_down)
        hn_f, norm_out_back = jax.vjp(lambda values: rms_scale(values, gain_out), h_res)
        hn_bf = hn_f.astype(jnp.bfloat16)
        logits = jnp.einsum("td,vd->tv", hn_bf, table_part, preferred_element_type=jnp.float32)
        row_max = lax.pmax(jnp.max(logits, axis=-1), "model")
        exp_shift = jnp.exp(logits - row_max[:, None])
        local_labels = tok_labels.reshape(local_count) - vocab_start
        onehot = lax.broadcasted_iota(jnp.int32, logits.shape, 1) == local_labels[:, None]
        part_stats = jnp.stack([jnp.sum(exp_shift, axis=-1), jnp.sum(jnp.where(onehot, logits, 0.0), axis=-1)])
        tok_stats = lax.psum(part_stats, "model")
        sum_exp = tok_stats[0]
        tok_loss = row_max + jnp.log(sum_exp) - tok_stats[1]
        loss = lax.psum(jnp.sum(tok_loss), "fsdp") / num_tokens
        soft_probs = exp_shift / sum_exp[:, None]
        d_logits = (jnp.where(onehot, soft_probs - 1.0, soft_probs) / num_tokens).astype(jnp.bfloat16)
        d_head = jnp.einsum("tv,td->vd", d_logits, hn_bf, preferred_element_type=jnp.float32)
        d_hn = lax.psum(jnp.einsum("tv,vd->td", d_logits, table_part, preferred_element_type=jnp.float32), "model")
        d_hidden = norm_out_back(d_hn)[0]
        d_x, grad_gate, grad_up, grad_down = mlp_backward(d_hidden, saved, w_gate, w_up, w_down)
        d_in = jax.ops.segment_sum(jnp.where(id_inside[:, None], d_x, 0.0), safe_ids, num_segments=vocab_part)
        grad_table = lax.psum_scatter(d_head + d_in, "fsdp", scatter_dimension=0, tiled=True)
        grad_gate = lax.psum_scatter(grad_gate, "fsdp", scatter_dimension=0, tiled=True)
        grad_up = lax.psum_scatter(grad_up, "fsdp", scatter_dimension=0, tiled=True)
        grad_down = lax.psum_scatter(grad_down, "fsdp", scatter_dimension=0, tiled=True)
        return loss, grad_table, grad_gate, grad_up, grad_down

    return jax.shard_map(device_step, mesh=mesh, in_specs=(tok_spec, tok_spec, row_spec, weight_spec, weight_spec, weight_spec, P(), P()), out_specs=(P(), row_spec, weight_spec, weight_spec, weight_spec), check_vma=False)
```

profile of v0, /device:TPU:0, one launch (start us, length us, event | category | flops | bytes accessed | tf_op | source)
XLA Modules:
  0.0 2001.0 jit_solution(9263294559246534321)
XLA Ops:
  8.6 211.0 %all-gather.12.cloned.1.call-done = bf16[4,4748,896]{2,1,0:T(8,128)(2,1)} async-done(((bf16[1,4748,896]{2,1,0:T(8,128)(2,1)}), bf16[4,4748,896]{2,1,0:T(8,128)(2,1)}) %all-gather.12.cloned.1.call-update) | async-done | bytes 34033680 | tf_op jit(solution)/shard_map/all_gather | solution.py:50
  219.6 29.8 %reshape.120 = bf16[18992,896]{1,0:T(8,128)(2,1)} reshape(bf16[4,4748,896]{2,1,0:T(8,128)(2,1)} %all-gather.12.cloned.1.call-done) | data formatting | bytes 68067328
  249.4 42.1 %gather_fusion = bf16[1024,896]{1,0:T(8,128)(2,1)S(1)} fusion(bf16[18992,896]{1,0:T(8,128)(2,1)} %reshape.120, s32[1024]{0:T(1024)S(1)} %broadcast_clamp_fusion), kind=kCustom, calls=%fused_computation | custom fusion | bytes 3674112 | tf_op jit(solution)/shard_map/jit(_take)/gather | solution.py:59
  298.8 94.2 %all-reduce.5.cloned.1.call-done = bf16[1024,896]{0,1:T(8,128)(2,1)} async-done(((bf16[1024,896]{0,1:T(8,128)(2,1)}), bf16[1024,896]{0,1:T(8,128)(2,1)}) %all-reduce.5.cloned.1.call-update) | async-done | bytes 1835024 | tf_op jit(solution)/shard_map/psum | solution.py:60
  395.5 58.7 %all-gather.6.cloned.1.call-done = bf16[896,4864]{1,0:T(8,128)(2,1)} async-done(((bf16[224,4864]{1,0:T(8,128)(2,1)}), bf16[896,4864]{1,0:T(8,128)(2,1)}) %all-gather.6.cloned.1.call-update) | async-done | bytes 8716304 | tf_op jit(solution)/shard_map/all_gather | solution.py:51
  454.3 17.1 convolution_convert_fusion.1
  471.4 44.7 %all-gather.8.cloned.1.call-done = bf16[896,4864]{1,0:T(8,128)(2,1)} async-done(((bf16[224,4864]{1,0:T(8,128)(2,1)}), bf16[896,4864]{1,0:T(8,128)(2,1)}) %all-gather.8.cloned.1.call-update) | async-done | bytes 8716304 | tf_op jit(solution)/shard_map/all_gather | solution.py:52
  516.1 23.9 %fusion.4 = (bf16[1024,4864]{1,0:T(8,128)(2,1)}, bf16[1024,4864]{1,0:T(8,128)(2,1)}) fusion(bf16[1024,4864]{1,0:T(8,128)(2,1)} %convolution_convert_fusion.1, bf16[896,4864]{1,0:T(8,128)(2,1)} %all-gather.8.cloned.1.call-done, bf16[1024,896]{0,1:T(8,128)(2,1)S(1)} %copy-done, f32[896]{0:T(1024)S(1)} %copy-done.23, f32[1024]{0:T(1024)S(1)} %fusion.22), kind=kOutput, calls=%fused_computation.14 | convolution fusion | flops 8973975552 | bytes 40443392 | tf_op jit(solution)/shard_map/dot_general | solution.py:18
  540.0 37.9 %all-gather.10.cloned.1.call-done = bf16[4864,896]{1,0:T(8,128)(2,1)} async-done(((bf16[1216,896]{1,0:T(8,128)(2,1)}), bf16[4864,896]{1,0:T(8,128)(2,1)}) %all-gather.10.cloned.1.call-update) | async-done | bytes 8716304 | tf_op jit(solution)/shard_map/all_gather | solution.py:53
  593.5 51.2 %fusion.33 = (f32[1024]{0:T(1024)S(1)}, f32[1024,18992]{0,1:T(8,128)}) fusion(bf16[18992,896]{1,0:T(8,128)(2,1)} %reshape.120, bf16[1024,896]{0,1:T(8,128)(2,1)} %get-tuple-element.19, bf16[1024,896]{0,1:T(8,128)(2,1)S(1)} %copy-done, f32[896]{0:T(1024)S(1)} %copy-done.9, f32[1024]{0:T(1024)S(1)} %fusion.23), kind=kOutput, calls=%fused_computation.70 | convolution fusion | flops 34875424768 | bytes 115506688 | tf_op jit(solution)/shard_map/td,vd->tv/dot_general | solution.py:64
  644.6 21.3 %pmax.7 = f32[1024]{0:T(1024)S(1)} all-reduce(f32[1024]{0:T(1024)S(1)} %get-tuple-element.20), channel_id=1, replica_groups=mesh['model'=8,'fsdp'=4] {'model'}, use_global_device_ids=true, to_apply=%region_4.5 | all-reduce | flops 1024 | bytes 8192 | tf_op jit(solution)/shard_map/pmax | solution.py:65
  666.0 24.8 %fusion.3 = (f32[1024]{0:T(1024)S(1)}, f32[1024]{0:T(1024)S(1)}) fusion(f32[1024,18992]{0,1:T(8,128)} %get-tuple-element.21, f32[1024]{0:T(1024)S(1)} %pmax.7, s32[1024]{0:T(1024)S(1)} %bitcast.33), kind=kLoop, calls=%fused_computation.8 | loop fusion | flops 97236992 | bytes 77807616 | tf_op jit(solution)/shard_map/reduce_sum | solution.py:69
  690.8 17.4 psum.29
  708.8 38.9 %fusion.2 = bf16[1024,18992]{0,1:T(8,128)(2,1)} fusion(f32[1024,18992]{0,1:T(8,128)} %get-tuple-element.21, f32[1024]{0:T(1024)S(1)} %bitcast.35, s32[1024]{0:T(1024)S(1)} %bitcast.34, f32[1024]{0:T(1024)S(1)} %pmax.7), kind=kLoop, calls=%fused_computation.4 | loop fusion | flops 136134656 | bytes 116699136 | tf_op jit(solution)/shard_map/convert_element_type | solution.py:75
  747.7 43.8 %fusion.34 = f32[1024,896]{0,1:T(8,128)} fusion(bf16[1024,18992]{0,1:T(8,128)(2,1)} %fusion.2, bf16[18992,896]{1,0:T(8,128)(2,1)} %reshape.120), kind=kOutput, calls=%fused_computation.71 | convolution fusion | flops 34850471936 | bytes 76599296 | tf_op jit(solution)/shard_map/tv,vd->td/dot_general | solution.py:77
  791.7 140.1 %all-reduce.7.cloned.1.call-done = f32[1024,896]{0,1:T(8,128)} async-done(((f32[1024,896]{0,1:T(8,128)}), f32[1024,896]{0,1:T(8,128)}) %all-reduce.7.cloned.1.call-update) | async-done | bytes 3670032 | tf_op jit(solution)/shard_map/psum | solution.py:77
  935.2 25.9 %multiply_convert_fusion = (bf16[1024,4864]{1,0:T(8,128)(2,1)}, bf16[1024,4864]{1,0:T(8,128)(2,1)}) fusion(bf16[1024,4864]{1,0:T(8,128)(2,1)} %convolution_convert_fusion.1, bf16[1024,4864]{1,0:T(8,128)(2,1)} %get-tuple-element.17, bf16[4864,896]{1,0:T(8,128)(2,1)} %all-gather.10.cloned.1.call-done, f32[1024]{0:T(1024)S(1)} %multiply_multiply_fusion.1, ...), kind=kOutput, calls=%fused_computation.22 | convolution fusion | flops 9008447488 | bytes 55913984 | tf_op jit(solution)/shard_map/td,fd->tf/dot_general | solution.py:30
  961.1 16.0 fusion.28
  977.2 16.0 fusion.26
  995.0 50.0 %fusion.24 = f32[18992,896]{1,0:T(8,128)} fusion(bf16[1024,18992]{0,1:T(8,128)(2,1)} %fusion.2, bf16[1024,896]{0,1:T(8,128)(2,1)} %get-tuple-element.19, bf16[1024,896]{0,1:T(8,128)(2,1)S(1)} %copy-done, f32[896]{0:T(1024)S(1)} %copy-done.9, f32[1024]{0:T(1024)S(1)} %fusion.23), kind=kOutput, calls=%fused_computation.65 | convolution fusion | flops 34855976960 | bytes 110640640 | tf_op jit(solution)/shard_map/tv,td->vd/dot_general | solution.py:76
  1082.3 18.8 fusion.18
  1101.8 152.9 %scatter_fusion = f32[18992,896]{1,0:T(8,128)} fusion(f32[18992,896]{1,0:T(8,128)} %fusion.24, s32[1024]{0:T(1024)S(1)} %bitcast.37, f32[1024,896]{1,0:T(8,128)} %copy.20), kind=kCustom, calls=%fused_computation.1 | custom fusion | flops 917504 | bytes 11014144 | tf_op jit(solution)/shard_map/scatter-add | solution.py:80
  1254.6 672.8 %fusion = f32[4752,896]{1,0:T(8,128)} fusion(f32[18992,896]{1,0:T(8,128)} %scatter_fusion), kind=kCustom, calls=%all-reduce-scatter | all-reduce-scatter fusion | flops 17031168 | bytes 85099008
  1939.0 42.1 %concatenate = f32[4764,896]{1,0:T(8,128)} concatenate(f32[12,896]{1,0:T(8,128)S(1)} %collective-permute-done, f32[4752,896]{1,0:T(8,128)} %fusion), dimensions={0} | concatenate | bytes 34148352
  (97 shorter events, 92.4 us)
Async XLA Ops:
  7.2 212.4 %all-gather.12.cloned.1.call-start = ((), (), s32[]{:S(2)}) async-start(), calls=%async_computation.11 | async-start | bytes 42577920 | tf_op jit(solution)/shard_map/all_gather | solution.py:50
  7.9 385.1 %all-reduce.5.cloned.1.call-start = ((), (), s32[]{:S(2)}) async-start(), calls=%async_computation.3 | async-start | bytes 3670016 | tf_op jit(solution)/shard_map/psum | solution.py:60
  8.6 285.3 %copy-start.18 = (pred[1024]{0:T(1024)(128)(4,1)}, pred[1024]{0:T(1024)(128)(4,1)S(1)}, u32[]{:S(2)}) copy-start(pred[1024]{0:T(1024)(128)(4,1)S(1)} %get-tuple-element.14) | copy-start | bytes 3076
  296.9 157.4 %copy-start.23 = (f32[896]{0:T(1024)S(1)}, f32[896]{0:T(1024)}, u32[]{:S(2)}) copy-start(f32[896]{0:T(1024)} %param.14) | copy-start | bytes 10756
  296.9 157.4 %all-gather.6.cloned.1.call-start = ((), (), s32[]{:S(2)}) async-start(), calls=%async_computation.4 | async-start | bytes 10895360 | tf_op jit(solution)/shard_map/all_gather | solution.py:51
  297.6 218.5 %all-gather.8.cloned.1.call-start = ((), (), s32[]{:S(2)}) async-start(), calls=%async_computation.5 | async-start | bytes 10895360 | tf_op jit(solution)/shard_map/all_gather | solution.py:52
  298.2 279.8 %all-gather.10.cloned.1.call-start = ((), (), s32[]{:S(2)}) async-start(), calls=%async_computation.6 | async-start | bytes 10895360 | tf_op jit(solution)/shard_map/all_gather | solution.py:53
  298.8 633.0 %all-reduce.7.cloned.1.call-start = ((), (), s32[]{:S(2)}) async-start(), calls=%async_computation.7 | async-start | bytes 7340032 | tf_op jit(solution)/shard_map/psum | solution.py:77
  395.5 120.6 %copy-start.12 = (f32[1024]{0:T(1024)}, f32[1024]{0:T(1024)S(1)}, u32[]{:S(2)}) copy-start(f32[1024]{0:T(1024)S(1)} %fusion.22) | copy-start | bytes 12292
  395.5 120.6 %copy-start = (bf16[1024,896]{0,1:T(8,128)(2,1)S(1)}, bf16[1024,896]{0,1:T(8,128)(2,1)}, u32[]{:S(2)}) copy-start(bf16[1024,896]{0,1:T(8,128)(2,1)} %all-reduce.5.cloned.1.call-done) | copy-start | bytes 5505028
  593.4 51.2 %copy-start.15 = (f32[1024]{0:T(1024)}, f32[1024]{0:T(1024)S(1)}, u32[]{:S(2)}) copy-start(f32[1024]{0:T(1024)S(1)} %get-tuple-element.18) | copy-start | bytes 12292
  666.0 42.8 %copy-start.3 = (f32[1024]{0:T(1024)}, f32[1024]{0:T(1024)S(1)}, u32[]{:S(2)}) copy-start(f32[1024]{0:T(1024)S(1)} %pmax.7) | copy-start | bytes 12292
  708.8 38.9 %copy-start.5 = (f32[1,1024]{1,0:T(1,128)}, f32[1,1024]{1,0:T(1,128)S(1)}, u32[]{:S(2)}) copy-start(f32[1,1024]{1,0:T(1,128)S(1)} %get-tuple-element.12) | copy-start | bytes 12292
  791.6 143.5 %copy-start.16 = (f32[1024]{0:T(1024)S(1)}, f32[1024]{0:T(1024)}, u32[]{:S(2)}) copy-start(f32[1024]{0:T(1024)} %copy-done.15) | copy-start | bytes 12292
  791.6 1201.3 %reduce-scatter.6.cloned.1.call-start = ((), (), s32[]{:S(2)}) async-start(), calls=%async_computation.8 | async-start | bytes 21790720 | tf_op jit(solution)/shard_map/reduce_scatter | solution.py:82
  935.2 25.9 %copy-start.10 = (f32[1024]{0:T(1024)}, f32[1024]{0:T(1024)S(1)}, u32[]{:S(2)}) copy-start(f32[1024]{0:T(1024)S(1)} %multiply_multiply_fusion.1) | copy-start | bytes 12292
  935.2 25.9 %copy-start.13 = (f32[1024]{0:T(1024)S(1)}, f32[1024]{0:T(1024)}, u32[]{:S(2)}) copy-start(f32[1024]{0:T(1024)} %copy-done.12) | copy-start | bytes 12292
  935.2 25.9 %copy-start.24 = (f32[896]{0:T(1024)S(1)}, f32[896]{0:T(1024)}, u32[]{:S(2)}) copy-start(f32[896]{0:T(1024)} %param.14) | copy-start | bytes 10756
  977.1 1015.8 %reduce-scatter.8.cloned.1.call-start = ((), (), s32[]{:S(2)}) async-start(), calls=%async_computation.9 | async-start | bytes 21790720 | tf_op jit(solution)/shard_map/reduce_scatter | solution.py:83
  993.2 999.8 %reduce-scatter.10.cloned.1.call-start = ((), (), s32[]{:S(2)}) async-start(), calls=%async_computation.10 | async-start | bytes 21790720 | tf_op jit(solution)/shard_map/reduce_scatter | solution.py:84
  1254.6 674.9 %copy-start.4 = (f32[1024]{0:T(1024)S(1)}, f32[1024]{0:T(1024)}, u32[]{:S(2)}) copy-start(f32[1024]{0:T(1024)} %copy-done.3) | copy-start | bytes 12292
  1254.6 674.9 %copy-start.6 = (f32[1,1024]{1,0:T(1,128)S(1)}, f32[1,1024]{1,0:T(1,128)}, u32[]{:S(2)}) copy-start(f32[1,1024]{1,0:T(1,128)} %copy-done.5) | copy-start | bytes 12292
  1254.6 674.9 %copy-start.17 = (f32[1,1024]{1,0:T(1,128)S(1)}, f32[1,1024]{1,0:T(1,128)}, u32[]{:S(2)}) copy-start(f32[1,1024]{1,0:T(1,128)} %get-tuple-element.13) | copy-start | bytes 12292
  1928.3 10.8 collective-permute-start
  (11 other events, 94.0 us)
Sparse Core Ops, SparseCore 0:
  9.6 209.9 all-gather.11
  297.0 96.0 all-reduce.4
  394.6 59.6 all-gather.5
  455.7 60.3 all-gather.7
  517.5 60.3 all-gather.9
  791.7 140.0 all-reduce.6
  977.2 127.4 reduce-scatter.5
  1107.9 128.2 reduce-scatter.7
  1239.4 222.8 reduce-scatter.9
where the time goes:
time: 2020 us; the launch traced here: 2000 us
  blocking collectives  720 us (36%)
  waiting for transfers between devices  589 us (29%)
  matrix products  307 us (15%)
  other arithmetic  230 us (11%)
  local copies, waits for them, and re-layouts  137 us (7%)
    unnamed x1, blocking collectives  673 us
    all_gather x1, waiting for transfers between devices, device_step(): table_part = lax.all_gather(table_shard, 'fsdp', axis=0, tiled=True)  211 us
    scatter-add x1, other arithmetic, device_step(): jax.ops.segment_sum(jnp.where(id_inside[:, None], d_x, 0.0), safe_ids, nu...  153 us
    psum x1, waiting for transfers between devices, device_step(): lax.psum(jnp.einsum('tv,vd->td', d_logits, table_part, preferred_element_...  140 us
    psum x1, waiting for transfers between devices, device_step(): x_emb = lax.psum(emb_rows, 'model').astype(jnp.float32)  94.2 us
    unnamed x55, local copies, waits for them, and re-layouts  87 us
    all_gather x1, waiting for transfers between devices, device_step(): w_gate = lax.all_gather(gate_shard, 'fsdp', axis=0, tiled=True)  58.7 us
    dot_general x1, matrix products, device_step(): jnp.einsum('td,vd->tv', hn_bf, table_part, preferred_element_type=jnp.flo...  51.2 us
  transfers between devices with their start and end apart: 10, of which 6 were waited for; matrix products, arithmetic and copies ran while one was open for 52% of the time, Pallas kernels for 0%

commit v1 on v0

v1 whole, which is shorter than its diff:
```python
import functools

import jax
import jax.numpy as jnp
from jax import lax
from jax.experimental import pallas as pl
from jax.experimental.pallas import tpu as pltpu
from jax.sharding import PartitionSpec as P

EPS = 1e-6
ALL = ("model", "fsdp")
SMEM = pltpu.MemorySpace.SMEM
BF = jnp.bfloat16
F32 = jnp.float32


def rms_scale(values, gain_vec):
    mean_sq = jnp.mean(values * values, axis=-1, keepdims=True)
    return values * lax.rsqrt(mean_sq + EPS) * gain_vec


def mlp_forward(x_emb, gain_in, w_gate, w_up, w_down):
    normed_in, norm_in_back = jax.vjp(lambda values: rms_scale(values, gain_in), x_emb)
    normed_bf = normed_in.astype(BF)
    gate_f = jnp.dot(normed_bf, w_gate, preferred_element_type=F32).astype(BF).astype(F32)
    up_f = jnp.dot(normed_bf, w_up, preferred_element_type=F32).astype(BF).astype(F32)
    gate_sig = jax.nn.sigmoid(gate_f)
    silu_gate = gate_f * gate_sig
    act_bf = (silu_gate * up_f).astype(BF)
    mlp_out = jnp.dot(act_bf, w_down, preferred_element_type=F32).astype(BF)
    h_res = x_emb + mlp_out.astype(F32)
    return h_res, (norm_in_back, normed_bf, gate_f, up_f, gate_sig, silu_gate)


def gather_rows(ids, base, table, table_tail):
    total = ids.shape[0]
    rows, width = table.shape
    depth = 64
    last_block = rows // 8 * 8

    def kernel(ids_ref, base_ref, table_ref, tail_ref, out_ref, token, held, wide, in_sem):
        start_row = base_ref[0]

        def scan(group, filled):
            for k in range(8):
                t = group * 8 + k
                row = ids_ref[t] - start_row
                token[filled] = t
                filled = filled + ((row >= 0) & (row < rows)).astype(jnp.int32)
            return filled

        filled = lax.fori_loop(0, total // 8, scan, 0)

        def row_of(j):
            return ids_ref[token[j]] - start_row

        def block_copy(j):
            block = jnp.minimum(row_of(j) // 8 * 8, last_block - 8)
            slot = lax.rem(j, depth)
            return pltpu.make_async_copy(table_ref.at[pl.ds(pl.multiple_of(block, 8), 8)], held.at[slot], in_sem.at[slot])

        def begin(j, _):
            block_copy(j).start()
            return 0

        lax.fori_loop(0, jnp.minimum(filled, depth), begin, 0)

        def clear(i, _):
            wide[pl.ds(pl.multiple_of(i * 64, 64), 64), :] = jnp.zeros((64, width), F32)
            return 0

        lax.fori_loop(0, total // 64, clear, 0)
        sublane = lax.broadcasted_iota(jnp.int32, (8, width), 0)

        def step(j, _):
            block_copy(j).wait()
            row = row_of(j)
            body = held[lax.rem(j, depth)].astype(F32)
            tail = tail_ref[...].astype(F32)
            in_tail = row >= last_block
            chosen = jnp.where(in_tail, row - (rows - 8), row - row // 8 * 8)
            block = jnp.where(in_tail, tail, body)
            wide[pl.ds(token[j], 1), :] = jnp.sum(jnp.where(sublane == chosen, block, 0.0), axis=0, keepdims=True)

            @pl.when(j + depth < filled)
            def _():
                block_copy(j + depth).start()

            return 0

        lax.fori_loop(0, filled, step, 0)

        def narrow(i, _):
            where = pl.ds(pl.multiple_of(i * 64, 64), 64)
            out_ref[where, :] = wide[where, :].astype(BF)
            return 0

        lax.fori_loop(0, total // 64, narrow, 0)

    smem = pl.BlockSpec(memory_space=SMEM)
    return pl.pallas_call(
        kernel,
        out_shape=jax.ShapeDtypeStruct((total, width), BF),
        in_specs=[smem, smem, pl.BlockSpec(memory_space=pl.ANY), pl.BlockSpec(memory_space=pltpu.VMEM)],
        out_specs=pl.BlockSpec(memory_space=pltpu.VMEM),
        scratch_shapes=[
            pltpu.SMEM((total + 8,), jnp.int32),
            pltpu.VMEM((depth, 8, width), BF),
            pltpu.VMEM((total + 8, width), F32),
            pltpu.SemaphoreType.DMA((depth,)),
        ],
        cost_estimate=pl.CostEstimate(flops=total * width * 100, bytes_accessed=total * width * 2, transcendentals=0),
        name="gather_rows",
    )(ids, base, table, table_tail)


def add_rows(ids, base, values, grad):
    total = ids.shape[0]
    rows, width = grad.shape
    block_rows = 512
    blocks = pl.cdiv(rows, block_rows)

    def kernel(ids_ref, base_ref, values_ref, grad_ref, out_ref, head, following, token, held, sem):
        block = pl.program_id(0)
        fetch = pltpu.make_async_copy(values_ref, held.at[pl.ds(0, total)], sem)

        @pl.when(block == 0)
        def _():
            fetch.start()
            start_row = base_ref[0]

            def clear(b, _):
                head[b] = -1
                return 0

            lax.fori_loop(0, blocks, clear, 0)

            def scan(group, filled):
                for k in range(8):
                    t = group * 8 + k
                    row = ids_ref[t] - start_row
                    token[filled] = t
                    filled = filled + ((row >= 0) & (row < rows)).astype(jnp.int32)
                return filled

            filled = lax.fori_loop(0, total // 8, scan, 0)

            def chain(j, _):
                owner = (ids_ref[token[j]] - start_row) // block_rows
                following[j] = head[owner]
                head[owner] = j
                return 0

            lax.fori_loop(0, filled, chain, 0)
            fetch.wait()

        out_ref[...] = grad_ref[...]
        block_start = base_ref[0] + block * block_rows
        sublane = lax.broadcasted_iota(jnp.int32, (8, width), 0)

        def add(j):
            t = token[j]
            row = ids_ref[t] - block_start
            where = pl.ds(pl.multiple_of(row // 8 * 8, 8), 8)
            out_ref[where, :] += jnp.where(sublane == row - row // 8 * 8, held[pl.ds(t, 1), :], 0.0)
            return following[j]

        lax.while_loop(lambda j: j >= 0, add, head[block])

    smem = pl.BlockSpec(memory_space=SMEM)
    block_spec = pl.BlockSpec((block_rows, width), lambda i: (i, 0))
    return pl.pallas_call(
        kernel,
        grid=(blocks,),
        out_shape=jax.ShapeDtypeStruct(grad.shape, F32),
        in_specs=[smem, smem, pl.BlockSpec(memory_space=pl.ANY), block_spec],
        out_specs=block_spec,
        scratch_shapes=[
            pltpu.SMEM((blocks,), jnp.int32),
            pltpu.SMEM((total,), jnp.int32),
            pltpu.SMEM((total + 8,), jnp.int32),
            pltpu.VMEM((total + 8, width), F32),
            pltpu.SemaphoreType.DMA,
        ],
        input_output_aliases={3: 0},
        cost_estimate=pl.CostEstimate(flops=total * width * 100, bytes_accessed=rows * width * 8, transcendentals=0),
        name="add_rows",
    )(ids, base, values, grad)


def solution(mesh):
    model_size, fsdp_size = mesh.shape["model"], mesh.shape["fsdp"]
    size = model_size * fsdp_size
    tok_spec = P("fsdp", None)
    row_spec = P(("model", "fsdp"), None)
    weight_spec = P("fsdp", None)

    def device_step(tok_ids, tok_labels, table, gate_shard, up_shard, down_shard, gain_in, gain_out):
        model_at, fsdp_at = lax.axis_index("model"), lax.axis_index("fsdp")
        me = model_at * fsdp_size + fsdp_at
        core, side = fsdp_at % 2, fsdp_at // 2
        local_count = tok_ids.shape[0] * tok_ids.shape[1]
        num_tokens = local_count * fsdp_size
        rows, width = table.shape
        hidden = gate_shard.shape[1]
        quarter, half = hidden // 4, hidden // 2

        both = jnp.stack([tok_ids.reshape(local_count), tok_labels.reshape(local_count)])
        both = lax.all_gather(both, "fsdp", axis=1, tiled=True)
        ids, labels = both[0], both[1]
        base = jnp.full((1,), me * rows, jnp.int32)
        x_emb = gather_rows(ids, base, table, table[rows - 8 :])
        x_emb = lax.psum_scatter(x_emb, ALL, scatter_dimension=0, tiled=True).astype(F32)

        w_gate = lax.all_gather(gate_shard, "fsdp", axis=0, tiled=True)
        w_up = lax.all_gather(up_shard, "fsdp", axis=0, tiled=True)
        w_down = lax.all_gather(down_shard, "fsdp", axis=0, tiled=True)

        h_res, (norm_in_back, a_mine, gate_f, up_f, gate_sig, silu_gate) = mlp_forward(x_emb, gain_in, w_gate, w_up, w_down)
        hn_f, norm_out_back = jax.vjp(lambda values: rms_scale(values, gain_out), h_res)
        hn = lax.all_gather(hn_f.astype(BF), ALL, axis=0, tiled=True)
        a_all = lax.all_gather(a_mine, ALL, axis=0, tiled=True)

        logits = jnp.einsum("td,vd->tv", hn, table, preferred_element_type=F32)
        row_max = lax.pmax(jnp.max(logits, axis=-1), ALL)
        exp_shift = jnp.exp(logits - row_max[:, None])
        local_labels = labels - me * rows
        onehot = lax.broadcasted_iota(jnp.int32, logits.shape, 1) == local_labels[:, None]
        part_stats = jnp.stack([jnp.sum(exp_shift, axis=-1), jnp.sum(jnp.where(onehot, logits, 0.0), axis=-1)])
        tok_stats = lax.psum(part_stats, ALL)
        sum_exp = tok_stats[0]
        tok_loss = row_max + jnp.log(sum_exp) - tok_stats[1]
        loss = jnp.sum(tok_loss) / num_tokens
        soft_probs = exp_shift / sum_exp[:, None]
        d_logits = (jnp.where(onehot, soft_probs - 1.0, soft_probs) / num_tokens).astype(BF)
        d_hn = jnp.einsum("tv,vd->td", d_logits, table, preferred_element_type=F32)
        d_hn = lax.psum_scatter(d_hn, ALL, scatter_dimension=0, tiled=True)
        d_head = jnp.einsum("tv,td->vd", d_logits, hn, preferred_element_type=F32)

        d_hidden = norm_out_back(d_hn)[0]
        d_mlp = d_hidden.astype(BF)
        d_act = jnp.einsum("td,fd->tf", d_mlp, w_down, preferred_element_type=F32)
        d_gate = (d_act * up_f * (gate_sig * (1.0 + gate_f * (1.0 - gate_sig)))).astype(BF)
        d_up = (d_act * silu_gate).astype(BF)
        d_normed = jnp.einsum("tf,df->td", d_gate, w_gate, preferred_element_type=F32) + jnp.einsum("tf,df->td", d_up, w_up, preferred_element_type=F32)
        d_x = d_hidden + norm_in_back(d_normed)[0]
        d_x_all = lax.all_gather(d_x, ALL, axis=0, tiled=True)
        grad_table = add_rows(ids, base, d_x_all, d_head)

        dm_all = lax.all_gather(d_mlp, ALL, axis=0, tiled=True)
        pick = lambda w: lax.dynamic_index_in_dim(w.reshape(width, 2, 2, quarter), core, axis=2, keepdims=False).reshape(width, half)
        gate_half, up_half = pick(w_gate), pick(w_up)
        down_half = lax.dynamic_index_in_dim(w_down.reshape(2, 2, quarter, width), core, axis=1, keepdims=False).reshape(half, width)
        gate_a = jnp.dot(a_all, gate_half, preferred_element_type=F32).astype(BF).astype(F32)
        up_a = jnp.dot(a_all, up_half, preferred_element_type=F32).astype(BF).astype(F32)
        sig_a = jax.nn.sigmoid(gate_a)
        silu_a = gate_a * sig_a
        act_a = (silu_a * up_a).astype(BF)
        d_act_a = jnp.einsum("td,fd->tf", dm_all, down_half, preferred_element_type=F32)
        d_gate_a = (d_act_a * up_a * (sig_a * (1.0 + gate_a * (1.0 - sig_a)))).astype(BF)
        d_up_a = (d_act_a * silu_a).astype(BF)
        chip_rows = width // 2
        a_chip = lax.dynamic_slice(a_all, (0, side * chip_rows), (num_tokens, chip_rows))
        act_own = lax.dynamic_slice(act_a, (0, side * quarter), (num_tokens, quarter))
        grad_down = jnp.einsum("tf,td->fd", act_own, dm_all, preferred_element_type=F32)
        swap = [(i, i ^ 1) for i in range(fsdp_size)]

        def finish(d_part):
            grad = jnp.einsum("td,tf->df", a_chip, d_part, preferred_element_type=F32)
            grad = grad.reshape(2, chip_rows // 2, half)
            kept = lax.dynamic_index_in_dim(grad, core, axis=0, keepdims=False)
            got = lax.ppermute(lax.dynamic_index_in_dim(grad, 1 - core, axis=0, keepdims=False), "fsdp", swap)
            low = jnp.where(core == 0, kept, got).reshape(chip_rows // 2, 2, 1, quarter)
            high = jnp.where(core == 0, got, kept).reshape(chip_rows // 2, 2, 1, quarter)
            return jnp.concatenate([low, high], axis=2).reshape(chip_rows // 2, hidden)

        return loss, grad_table, finish(d_gate_a), finish(d_up_a), grad_down

    return jax.shard_map(device_step, mesh=mesh, in_specs=(tok_spec, tok_spec, row_spec, weight_spec, weight_spec, weight_spec, P(), P()), out_specs=(P(), row_spec, weight_spec, weight_spec, weight_spec), check_vma=False)
```

time: 2020 us -> 1260 us (0.62)
  blocking collectives: 720 us -> 86.2 us
  other arithmetic: 230 us -> 96.9 us
  matrix products: 307 us -> 373 us
  Pallas kernels: 0 us -> 60.9 us
  local copies, waits for them, and re-layouts: 137 us -> 80.6 us
  waiting for transfers between devices: 589 us -> 536 us
    unnamed x1 -> x0, blocking collectives: 673 us -> none
    reduce_scatter x3 -> x2, waiting for transfers between devices: 0.01 us -> 389 us  [the longest x1 266 us: device_step(): lax.psum_scatter(x_emb, ALL, scatter_dimension=0, tiled=True).astype(F32)]
    psum x2 -> x0, waiting for transfers between devices: 234 us -> none  [the longest x1 140 us: device_step(): lax.psum(jnp.einsum('tv,vd->td', d_logits, table_part, preferred_element_...]
    scatter-add x1 -> x0, other arithmetic: 153 us -> none  [device_step(): jax.ops.segment_sum(jnp.where(id_inside[:, None], d_x, 0.0), safe_ids, nu...]
    unnamed x55 -> x78, local copies, waits for them, and re-layouts: 87 us -> 1.45 us
    dot_general x12 -> x15, matrix products: 307 us -> 373 us  [the longest x2 67.3 us: finish(): grad = jnp.einsum('td,tf->df', a_chip, d_part, preferred_element_type=F32)]
    all_gather x1 -> x4, waiting for transfers between devices: 211 us -> 145 us  [the longest x1 73.1 us: device_step(): a_all = lax.all_gather(a_mine, ALL, axis=0, tiled=True)]
    pallas_call x0 -> x2, Pallas kernels: none -> 60.9 us  [the longest x1 33.9 us: add_rows(): pl.pallas_call(kernel, grid=(blocks,), out_shape=jax.ShapeDtypeStruct(gra...]
  transfers between devices with their start and end apart: 10 -> 11, of which waited for: 6 -> 4; matrix products, arithmetic and copies ran while one was open for 52% -> 30% of each run, Pallas kernels for 0% -> 0%
where the time goes in v1:
time: 1260 us; the launch traced here: 1250 us
  waiting for transfers between devices  536 us (43%)
  matrix products  373 us (30%)
  other arithmetic  96.9 us (8%)
  blocking collectives  86.2 us (7%)
  local copies, waits for them, and re-layouts  80.6 us (6%)
  Pallas kernels  60.9 us (5%)
  between operations  18.6 us (1%)
    reduce_scatter x1, waiting for transfers between devices, device_step(): lax.psum_scatter(x_emb, ALL, scatter_dimension=0, tiled=True).astype(F32)  266 us
    reduce_scatter x1, waiting for transfers between devices, device_step(): d_hn = lax.psum_scatter(d_hn, ALL, scatter_dimension=0, tiled=True)  124 us
    all_gather x1, waiting for transfers between devices, device_step(): a_all = lax.all_gather(a_mine, ALL, axis=0, tiled=True)  73.1 us
    all_gather x1, waiting for transfers between devices, device_step(): hn = lax.all_gather(hn_f.astype(BF), ALL, axis=0, tiled=True)  71.6 us
    dot_general x2, matrix products, finish(): grad = jnp.einsum('td,tf->df', a_chip, d_part, preferred_element_type=F32)  67.3 us
    dot_general x1, matrix products, device_step(): d_hn = jnp.einsum('tv,vd->td', d_logits, table, preferred_element_type=F32)  50.4 us
    dot_general x1, matrix products, device_step(): logits = jnp.einsum('td,vd->tv', hn, table, preferred_element_type=F32)  49.8 us
    dot_general x1, matrix products, device_step(): d_head = jnp.einsum('tv,td->vd', d_logits, hn, preferred_element_type=F32)  48.1 us
  transfers between devices with their start and end apart: 11, of which 4 were waited for; matrix products, arithmetic and copies ran while one was open for 30% of the time, Pallas kernels for 0%

profile of v1, /device:TPU:0, one launch (start us, length us, event | category | flops | bytes accessed | tf_op | source)
XLA Modules:
  0.0 1253.3 jit_solution(8092735002652729819)
XLA Ops:
  16.9 27.0 %gather_rows.1 = bf16[4096,896]{1,0:T(8,128)(2,1)} custom-call(s32[4096]{0:T(1024)} %bitcast.65, s32[1]{0:T(128)} %bitcast.1.base_ref, bf16[4748,896]{1,0:T(8,128)(2,1)} %table_ref.1, bf16[8,896]{1,0:T(8,128)(2,1)} %slice.16.tail_ref), custom_call_target="tpu_custom_call" | custom-call | flops 367001600 | bytes 7340032 | tf_op jit(solution)/shard_map/gather_rows/pallas_call | solution.py:101
  45.8 265.6 %reduce-scatter.3.cloned.1.call-done = bf16[128,896]{1,0:T(8,128)(2,1)} async-done(((bf16[4096,896]{1,0:T(8,128)(2,1)}), bf16[128,896]{1,0:T(8,128)(2,1)}) %reduce-scatter.3.cloned.1.call-update) | async-done | bytes 229392 | tf_op jit(solution)/shard_map/reduce_scatter | solution.py:213
  333.7 71.6 %all-gather.14.cloned.1.call-done = bf16[4096,896]{1,0:T(8,128)(2,1)} async-done(((bf16[128,896]{1,0:T(8,128)(2,1)}), bf16[4096,896]{1,0:T(8,128)(2,1)}) %all-gather.14.cloned.1.call-update) | async-done | bytes 7340048 | tf_op jit(solution)/shard_map/all_gather | solution.py:221
  405.2 49.8 %fusion.48 = (f32[4096]{0:T(1024)S(1)}, f32[4096,4748]{0,1:T(8,128)}) fusion(bf16[4096,896]{1,0:T(8,128)(2,1)} %all-gather.14.cloned.1.call-done, bf16[4748,896]{1,0:T(8,128)(2,1)} %table_ref.1), kind=kOutput, calls=%fused_computation.89 | convolution fusion | flops 34869915648 | bytes 93656064 | tf_op jit(solution)/shard_map/td,vd->tv/dot_general | solution.py:224
  455.1 39.4 %pmax.7 = f32[4096]{0:T(1024)S(1)} all-reduce(f32[4096]{0:T(1024)S(1)} %get-tuple-element.17), channel_id=1, replica_groups=mesh['model'=8,'fsdp'=4] {'model','fsdp'}, use_global_device_ids=true, to_apply=%region_4.5 | all-reduce | flops 4096 | bytes 32768 | tf_op jit(solution)/shard_map/pmax | solution.py:225
  494.5 24.8 %fusion.2 = (f32[4096]{0:T(1024)S(1)}, f32[4096]{0:T(1024)S(1)}) fusion(f32[4096,4748]{0,1:T(8,128)} %get-tuple-element.18, f32[4096]{0:T(1024)S(1)} %pmax.7, s32[4096]{0:T(1024)S(1)} %bitcast.69), kind=kLoop, calls=%fused_computation.6 | loop fusion | flops 97230848 | bytes 77856768 | tf_op jit(solution)/shard_map/reduce_sum | solution.py:229
  519.3 40.6 %psum.7 = f32[2,4096]{1,0:T(2,128)S(1)} all-reduce(f32[2,4096]{1,0:T(2,128)S(1)} %pad_maximum_fusion.2), channel_id=1, replica_groups=mesh['model'=8,'fsdp'=4] {'model','fsdp'}, use_global_device_ids=true, to_apply=%region_7.8 | all-reduce | flops 8192 | bytes 65536 | tf_op jit(solution)/shard_map/psum | solution.py:230
  560.6 38.6 %fusion.1 = bf16[4096,4748]{0,1:T(8,128)(2,1)} fusion(f32[4096,4748]{0,1:T(8,128)} %get-tuple-element.18, f32[4096]{0:T(1024)S(1)} %bitcast.67, s32[4096]{0:T(1024)S(1)} %bitcast.70, f32[4096]{0:T(1024)S(1)} %pmax.7), kind=kLoop, calls=%fused_computation.2 | loop fusion | flops 136134656 | bytes 116736000 | tf_op jit(solution)/shard_map/convert_element_type | solution.py:235
  599.2 50.4 %fusion.49 = f32[4096,896]{1,0:T(8,128)} fusion(bf16[4096,4748]{0,1:T(8,128)(2,1)} %fusion.1, bf16[4748,896]{1,0:T(8,128)(2,1)} %table_ref.1), kind=kOutput, calls=%fused_computation.90 | convolution fusion | flops 34850471936 | bytes 62084096 | tf_op jit(solution)/shard_map/tv,vd->td/dot_general | solution.py:236
  650.4 12.4 copy.22
  662.9 12.4 copy.20
  687.8 123.6 %reduce-scatter.5.cloned.1.call-done = f32[128,896]{1,0:T(8,128)} async-done(((f32[4096,896]{1,0:T(8,128)}), f32[128,896]{1,0:T(8,128)}) %reduce-scatter.5.cloned.1.call-update) | async-done | bytes 458768 | tf_op jit(solution)/shard_map/reduce_scatter | solution.py:237
  815.0 73.1 %all-gather.18.cloned.1.call-done = bf16[4096,896]{1,0:T(8,128)(2,1)} async-done(((bf16[128,896]{1,0:T(8,128)(2,1)}), bf16[4096,896]{1,0:T(8,128)(2,1)}) %all-gather.18.cloned.1.call-update) | async-done | bytes 7340048 | tf_op jit(solution)/shard_map/all_gather | solution.py:222
  888.2 35.2 %convert_multiply_fusion = (f32[4096,2432]{1,0:T(8,128)}, bf16[4096,2432]{1,0:T(8,128)(2,1)}) fusion(bf16[4096,896]{1,0:T(8,128)(2,1)} %all-gather.18.cloned.1.call-done, bf16[896,2432]{0,1:T(8,128)(2,1)} %bitcast.58), kind=kOutput, calls=%fused_computation.7 | convolution fusion | flops 17910726656 | bytes 71467008 | tf_op jit(solution)/shard_map/dot_general | solution.py:254
  924.6 28.8 %fusion.10 = f32[4096,2432]{1,0:T(8,128)} fusion(bf16[4096,896]{1,0:T(8,128)(2,1)} %all-gather.18.cloned.1.call-done, bf16[896,2432]{0,1:T(8,128)(2,1)} %bitcast.57), kind=kOutput, calls=%fused_computation.20 | convolution fusion | flops 17870880768 | bytes 51544064 | tf_op jit(solution)/shard_map/dot_general | solution.py:255
  953.5 48.1 %fusion.51.grad_ref = f32[4748,896]{1,0:T(8,128)} fusion(bf16[4096,4748]{0,1:T(8,128)(2,1)} %fusion.1, bf16[4096,896]{1,0:T(8,128)(2,1)} %all-gather.14.cloned.1.call-done), kind=kOutput, calls=%fused_computation.92 | convolution fusion | flops 34850471936 | bytes 63252480 | tf_op jit(solution)/shard_map/tv,td->vd/dot_general | solution.py:238
  1018.3 29.2 %fusion.52 = f32[4096,2432]{1,0:T(8,128)} fusion(bf16[4096,896]{1,0:T(8,128)(2,1)} %all-gather.20.cloned.1.call-done, bf16[2432,896]{1,0:T(8,128)(2,1)} %bitcast.56), kind=kOutput, calls=%fused_computation.93 | convolution fusion | flops 17850957824 | bytes 51544064 | tf_op jit(solution)/shard_map/td,fd->tf/dot_general | solution.py:259
  1047.4 39.1 %fusion.13 = f32[448,2432]{1,0:T(8,128)} fusion(bf16[4096,2432]{1,0:T(8,128)(2,1)} %get-tuple-element.22, f32[4096,2432]{1,0:T(8,128)} %fusion.52, f32[4096,2432]{1,0:T(8,128)} %fusion.10, bf16[4096,896]{1,0:T(8,128)(2,1)} %all-gather.18.cloned.1.call-done, s32[]{:T(128)S(6)} %select_n.64), kind=kOutput, calls=%fused_computation.24 | convolution fusion | flops 9035055104 | bytes 108167168 | tf_op jit(solution)/shard_map/td,tf->df/dot_general | solution.py:269
  1088.6 28.2 %fusion.12 = f32[448,2432]{1,0:T(8,128)S(1)} fusion(f32[4096,2432]{1,0:T(8,128)} %fusion.52, bf16[4096,896]{1,0:T(8,128)(2,1)} %all-gather.18.cloned.1.call-done, s32[]{:T(128)S(6)} %select_n.64, bf16[4096,2432]{1,0:T(8,128)(2,1)} %get-tuple-element.22), kind=kOutput, calls=%fused_computation.23 | convolution fusion | flops 8995209216 | bytes 68321280 | tf_op jit(solution)/shard_map/td,tf->df/dot_general | solution.py:269
  1118.6 30.4 %fusion.15 = f32[1216,896]{1,0:T(8,128)} fusion(bf16[4096,896]{1,0:T(8,128)(2,1)} %all-gather.20.cloned.1.call-done, f32[4096,2432]{1,0:T(8,128)} %fusion.10, s32[]{:T(128)S(6)} %select_n.71, f32[4096,2432]{1,0:T(8,128)} %get-tuple-element.21), kind=kOutput, calls=%fused_computation.25 | convolution fusion | flops 8935440384 | bytes 53641220 | tf_op jit(solution)/shard_map/tf,td->fd/dot_general | solution.py:265
  1164.0 8.0 pad_maximum_fusion
  1171.9 7.4 reshape.107
  1194.9 8.0 pad_maximum_fusion.1
  1210.2 33.9 %add_rows.1 = f32[4748,896]{1,0:T(8,128)} custom-call(s32[4096]{0:T(1024)} %bitcast.66, s32[1]{0:T(128)} %bitcast.1.base_ref, f32[4096,896]{1,0:T(8,128)} %all-gather.16.cloned.1.call-done.values_ref, f32[4748,896]{1,0:T(8,128)} %fusion.51.grad_ref), custom_call_target="tpu_custom_call", output_to_operand_aliasing={{}: (3, {})} | custom-call | flops 367001600 | bytes 34033664 | tf_op jit(solution)/shard_map/add_rows/pallas_call | solution.py:172
  (144 shorter events, 109.1 us)
Async XLA Ops:
  8.0 303.3 %reduce-scatter.3.cloned.1.call-start = ((), (), s32[]{:S(2)}) async-start(), calls=%async_computation.2 | async-start | bytes 7569408 | tf_op jit(solution)/shard_map/reduce_scatter | solution.py:213
  44.0 268.5 %copy-start.18 = (f32[896]{0:T(1024)S(1)}, f32[896]{0:T(1024)}, u32[]{:S(2)}) copy-start(f32[896]{0:T(1024)} %param.14) | copy-start | bytes 10756
  44.0 269.6 %all-gather.10.cloned.1.call-start = ((), (), s32[]{:S(2)}) async-start(), calls=%async_computation.4 | async-start | bytes 10895360 | tf_op jit(solution)/shard_map/all_gather | solution.py:216
  44.6 274.0 %all-gather.8.cloned.1.call-start = ((), (), s32[]{:S(2)}) async-start(), calls=%async_computation.3 | async-start | bytes 10895360 | tf_op jit(solution)/shard_map/all_gather | solution.py:215
  45.2 280.8 %all-gather.12.cloned.1.call-start = ((), (), s32[]{:S(2)}) async-start(), calls=%async_computation.5 | async-start | bytes 10895360 | tf_op jit(solution)/shard_map/all_gather | solution.py:217
  45.7 359.5 %all-gather.14.cloned.1.call-start = ((), (), s32[]{:S(2)}) async-start(), calls=%async_computation.6 | async-start | bytes 7569408 | tf_op jit(solution)/shard_map/all_gather | solution.py:221
  333.6 477.8 %reduce-scatter.5.cloned.1.call-start = ((), (), s32[]{:S(2)}) async-start(), calls=%async_computation.7 | async-start | bytes 15138816 | tf_op jit(solution)/shard_map/reduce_scatter | solution.py:237
  649.6 238.6 %all-gather.18.cloned.1.call-start = ((), (), s32[]{:S(2)}) async-start(), calls=%async_computation.9 | async-start | bytes 7569408 | tf_op jit(solution)/shard_map/all_gather | solution.py:222
  650.1 368.1 %all-gather.20.cloned.1.call-start = ((), (), s32[]{:S(2)}) async-start(), calls=%async_computation.10 | async-start | bytes 7569408 | tf_op jit(solution)/shard_map/all_gather | solution.py:250
  680.3 131.1 %copy-start.1 = (f32[128,896]{1,0:T(8,128)S(1)}, f32[128,896]{1,0:T(8,128)}, u32[]{:S(2)}) copy-start(f32[128,896]{1,0:T(8,128)} %copy-done) | copy-start | bytes 1376260
  680.3 131.1 %copy-start.12 = (f32[896]{0:T(1024)S(1)}, f32[896]{0:T(1024)}, u32[]{:S(2)}) copy-start(f32[896]{0:T(1024)} %param.15) | copy-start | bytes 10756
  680.3 132.3 %copy-start.27 = (f32[128]{0:T(128)S(1)}, f32[128]{0:T(128)}, u32[]{:S(2)}) copy-start(f32[128]{0:T(128)} %copy-done.26) | copy-start | bytes 1540
  680.3 132.9 %copy-start.16 = (f32[128]{0:T(128)S(1)}, f32[128]{0:T(128)}, u32[]{:S(2)}) copy-start(f32[128]{0:T(128)} %copy-done.15) | copy-start | bytes 1540
  815.0 395.2 %all-gather.16.cloned.1.call-start = ((), (), s32[]{:S(2)}) async-start(), calls=%async_computation.8 | async-start | bytes 15138816 | tf_op jit(solution)/shard_map/all_gather | solution.py:247
  888.2 35.2 %copy-start.14 = (f32[1,4096]{1,0:T(1,128)S(1)}, f32[1,4096]{1,0:T(1,128)}, u32[]{:S(2)}) copy-start(f32[1,4096]{1,0:T(1,128)} %get-tuple-element.12) | copy-start | bytes 49156
  924.6 83.0 %slice-start = ((s8[8716288]{0:T(1024)(128)(4,1)}), s8[327680]{0:T(1024)(128)(4,1)S(1)}, s32[]{:S(2)}) async-start(s8[8716288]{0:T(1024)(128)(4,1)} %bitcast.47), calls=%async_computation.11 | async-start | bytes 655360
  953.5 48.1 %copy-start.10 = (bf16[128,896]{1,0:T(8,128)(2,1)S(1)}, bf16[128,896]{1,0:T(8,128)(2,1)}, u32[]{:S(2)}) copy-start(bf16[128,896]{1,0:T(8,128)(2,1)} %fusion.46) | copy-start | bytes 688132
  953.5 54.2 %slice-start.1 = ((s8[8716288]{0:T(1024)(128)(4,1)}), s8[4194304]{0:T(1024)(128)(4,1)S(1)}, s32[]{:S(2)}) async-start(s8[8716288]{0:T(1024)(128)(4,1)} %bitcast.47), calls=%async_computation.12 | async-start | bytes 8388608
  953.5 54.2 %slice-start.2 = ((s8[8716288]{0:T(1024)(128)(4,1)}), s8[4194304]{0:T(1024)(128)(4,1)S(1)}, s32[]{:S(2)}) async-start(s8[8716288]{0:T(1024)(128)(4,1)} %bitcast.47), calls=%async_computation.13 | async-start | bytes 8388608
  1088.3 60.8 %collective-permute-start = (f32[224,2432]{1,0:T(8,128)S(1)}, f32[224,2432]{1,0:T(8,128)}, u32[]{:S(2)}, u32[]{:S(2)}) collective-permute-start(f32[224,2432]{1,0:T(8,128)S(1)} %dynamic-slice_bitcast_fusion.1), channel_id=1, source_target_pairs={{0,1},{1,0},{2,3},{3,2},{4,5},{5,4},{6,7},{7,6},{8,9},{9,8},{10,11... | collective-permute-start | bytes 6537224 | tf_op jit(solution)/shard_map/ppermute | solution.py:272
  1116.8 32.3 %copy-start.4 = (f32[448,2432]{1,0:T(8,128)}, f32[448,2432]{1,0:T(8,128)S(1)}, u32[]{:S(2)}) copy-start(f32[448,2432]{1,0:T(8,128)S(1)} %fusion.12) | copy-start | bytes 13074436
  1116.8 32.3 %slice-start.9 = ((s8[4358144]{0:T(1024)(128)(4,1)}), s8[4194304]{0:T(1024)(128)(4,1)S(1)}, s32[]{:S(2)}) async-start(s8[4358144]{0:T(1024)(128)(4,1)} %bitcast.62), calls=%async_computation.20 | async-start | bytes 8388608
  1118.3 61.0 %collective-permute-start.1 = (f32[224,2432]{1,0:T(8,128)}, f32[224,2432]{1,0:T(8,128)}, u32[]{:S(2)}, u32[]{:S(2)}) collective-permute-start(f32[224,2432]{1,0:T(8,128)} %dynamic-slice_bitcast_fusion), channel_id=1, source_target_pairs={{0,1},{1,0},{2,3},{3,2},{4,5},{5,4},{6,7},{7,6},{8,9},{9,8},{10,11... | collective-permute-start | bytes 6537224 | tf_op jit(solution)/shard_map/ppermute | solution.py:272
  1118.6 30.4 %slice-start.10 = ((s8[4358144]{0:T(1024)(128)(4,1)}), s8[163840]{0:T(1024)(128)(4,1)S(1)}, s32[]{:S(2)}) async-start(s8[4358144]{0:T(1024)(128)(4,1)} %bitcast.62), calls=%async_computation.21 | async-start | bytes 327680
  (26 other events, 132.2 us)
Sparse Core Ops, SparseCore 0:
  44.1 267.1 reduce-scatter.2
  333.7 71.4 all-gather.13
  649.7 161.6 reduce-scatter.4
  814.1 74.0 all-gather.17
  890.8 72.3 all-gather.19
  1018.3 105.4 all-gather.15
Sparse Core Ops, SparseCore 1:
  46.0 63.5 all-gather.9
  111.0 64.5 all-gather.7
  176.9 63.7 all-gather.11
